TPU v7x, 32 devices: a whole 2x2x4 slice. The times are simulated.
32 devices in a mesh: seg: 32 (over z, y, x, core).
Axes of the slice: x: 2, y: 2, z: 4, core: 2. Of those that a mesh axis runs over, the one named last changes fastest.
Arguments:
- tokens: bfloat16 [8192, 3584], P('seg'), may hold values from -6 to 6
- memory: bfloat16 [64, 3584], replicated, may hold values from -6 to 6
- norm_gain: float32 [3584], replicated, may hold values from 0.5 to 2
- post_gain: float32 [3584], replicated, may hold values from 0.5 to 2
- query_weight: bfloat16 [3584, 2048], P('seg'), may hold values from -0.09375 to 0.09375
- key_matrix: bfloat16 [3584, 1024], replicated, may hold values from -0.09375 to 0.09375
- value_matrix: bfloat16 [3584, 1024], replicated, may hold values from -0.09375 to 0.09375
- output_weight: bfloat16 [2048, 3584], P('seg'), may hold values from -0.125 to 0.125
- segment_weight: float32 [32], P('seg'), may hold values from 0.1 to 4
Outputs:
- token_out: bfloat16 [8192, 3584], P('seg')
- memory_out: bfloat16 [2048, 3584], P('seg')
- changes: float32 [3], replicated
All inputs are finite; a program needn't handle non-finite values.
Results may differ from a plain program's by a relative error of at most 0.014.
Values may be sent and summed in bfloat16 or wider, within the bound.
A program may use at most 192 MiB of HBM per device.

v0:
```python
import jax
import jax.numpy as jnp
from jax import lax
from jax.sharding import PartitionSpec as P

HEAD_WIDTH = 256
KEY_VALUE_HEADS = 4
ITERS = 3


eps = 1e-06


def from_behind(block, axis, distance):
    devices = range(lax.axis_size(axis))
    route = [(i - distance, i) for i in devices if i - distance in devices]
    return lax.ppermute(block, axis, route)


def prenorm(rows, gain):
    rows = rows.astype(jnp.float32)
    mean_sq = jnp.mean(rows * rows, axis=-1, keepdims=True)
    return (rows / jnp.sqrt(mean_sq + eps) * gain).astype(jnp.bfloat16)


def partial_attend(query_vectors, key_vectors, value_vectors, allowed):
    element_count = query_vectors.shape[0]
    feature_width = key_vectors.shape[0]
    query_heads_split = query_vectors.reshape(element_count, KEY_VALUE_HEADS, 2, HEAD_WIDTH)
    key_heads_split = key_vectors.reshape(feature_width, KEY_VALUE_HEADS, HEAD_WIDTH)
    value_heads_split = value_vectors.reshape(feature_width, KEY_VALUE_HEADS, HEAD_WIDTH)
    score = jnp.einsum(
        "rgjd,kgd->gjrk", query_heads_split, key_heads_split, preferred_element_type=jnp.float32
    )
    expo = jnp.exp(score)
    if allowed is not None:
        expo = jnp.where(allowed[None, None], expo, 0.0)
    denom = jnp.transpose(jnp.sum(expo, axis=-1), (2, 0, 1))
    numer = jnp.einsum(
        "gjrk,kgd->rgjd",
        expo.astype(jnp.bfloat16),
        value_heads_split,
        preferred_element_type=jnp.float32,
    )
    return (numer, denom)


def finish(inputs, numer, denom, output_weight, post_gain):
    element_count = numer.shape[0]
    attn = (numer / denom[:, :, :, None]).reshape(element_count, -1).astype(jnp.bfloat16)
    proj = jnp.dot(attn, output_weight, preferred_element_type=jnp.float32)
    mean_sq = jnp.mean(proj * proj, axis=-1, keepdims=True)
    return (inputs.astype(jnp.float32) + proj / jnp.sqrt(mean_sq + eps) * post_gain).astype(
        jnp.bfloat16
    )


def shards(
    tokens,
    memory,
    norm_gain,
    post_gain,
    query_weight,
    key_matrix,
    value_matrix,
    output_weight,
    segment_weight,
):
    tok_rows = tokens.shape[0]
    mem_rows = memory.shape[0]
    feature_width = memory.shape[1]
    inputs = jnp.concatenate([tokens, memory], axis=0)
    normed = prenorm(inputs, norm_gain)
    scale = 1.0 / HEAD_WIDTH**0.5
    query_acc = jnp.dot(
        normed,
        lax.all_gather(query_weight, "seg", axis=0, tiled=True),
        preferred_element_type=jnp.float32,
    )
    output_full = lax.all_gather(output_weight, "seg", axis=0, tiled=True)
    query_vectors = (query_acc * scale).astype(jnp.bfloat16)
    local_k = jnp.dot(normed, key_matrix, preferred_element_type=jnp.float32).astype(jnp.bfloat16)
    local_v = jnp.dot(normed, value_matrix, preferred_element_type=jnp.float32).astype(jnp.bfloat16)
    total_rows = tok_rows + mem_rows
    causal = jnp.tril(jnp.ones((total_rows, total_rows), bool))
    self_num, self_den = partial_attend(query_vectors, local_k, local_v, causal)
    first = jnp.int32(0) == lax.axis_index("seg")
    read = memory
    previous = memory
    squares = []
    result = inputs
    own_weight = segment_weight[0]
    count_all = lax.axis_size("seg") * mem_rows * feature_width
    for step in range(ITERS):
        read_norm = prenorm(read, norm_gain)
        read_k = jnp.dot(read_norm, key_matrix, preferred_element_type=jnp.float32).astype(
            jnp.bfloat16
        )
        read_v = jnp.dot(read_norm, value_matrix, preferred_element_type=jnp.float32).astype(
            jnp.bfloat16
        )
        if step + 1 == ITERS:
            mem_num, mem_den = partial_attend(query_vectors, read_k, read_v, None)
            result = finish(inputs, self_num + mem_num, self_den + mem_den, output_full, post_gain)
            newest = result[tok_rows:]
        else:
            mem_num, mem_den = partial_attend(query_vectors[tok_rows:], read_k, read_v, None)
            newest = finish(
                memory,
                self_num[tok_rows:] + mem_num,
                self_den[tok_rows:] + mem_den,
                output_full,
                post_gain,
            )
        diff = newest.astype(jnp.float32) - previous.astype(jnp.float32)
        local_sq = jnp.sum(diff * diff) * own_weight
        squares.append(local_sq)
        previous = newest
        if step + 1 < ITERS:
            shifted = from_behind(newest, "seg", 1)
            read = jnp.where(first, memory, shifted)
    totals = lax.psum(jnp.stack(squares), "seg")
    change_vec = jnp.sqrt(totals / count_all + eps)
    return (result[:tok_rows], previous, change_vec)


def solution(mesh):
    return jax.shard_map(
        shards,
        mesh=mesh,
        in_specs=(
            P("seg", None),
            P(),
            P(),
            P(),
            P("seg", None),
            P(),
            P(),
            P("seg", None),
            P("seg"),
        ),
        out_specs=(P("seg", None), P("seg", None), P()),
        check_vma=False,
    )
```

profile of v0, /device:TPU:0, one launch (start us, length us, event | category | flops | bytes accessed | tf_op | source)
XLA Modules:
  0.0 369.1 jit_solution(3991564716048365334)
XLA Ops:
  7.2 0.7 all-gather.3.cloned.1.call-update
  7.9 0.7 all-gather.5.cloned.1.call-update
  8.6 2.2 fusion
  10.9 6.4 %convolution_convert_fusion = bf16[320,1024]{1,0:T(8,128)(2,1)S(1)} fusion(bf16[3584,1024]{1,0:T(8,128)(2,1)} %param.14, f32[3584]{0:T(1024)} %param.11, f32[320]{0:T(512)S(1)} %add_sqrt_fusion.1, bf16[64,3584]{1,0:T(8,128)(2,1)} %param.10, bf16[256,3584]{1,0:T(8,128)(2,1)} %param.9), kind=kOutput, calls=%fused_computation.26 | convolution fusion | flops 2357166080 | bytes 10304768 | tf_op jit(solution)/shard_map/dot_general | solution.py:82
  17.3 0.5 reshape.113
  17.8 0.2 fusion.38
  18.0 4.7 %convolution_convert_fusion.6 = bf16[64,1024]{1,0:T(8,128)(2,1)S(1)} fusion(bf16[3584,1024]{1,0:T(8,128)(2,1)} %param.14, bf16[64,3584]{1,0:T(8,128)(2,1)S(1)} %copy-done, f32[3584]{0:T(1024)S(1)} %copy-done.10, f32[64]{0:T(128)S(1)} %add_sqrt_fusion.7), kind=kOutput, calls=%fused_computation.49 | convolution fusion | flops 470745088 | bytes 7944448 | tf_op jit(solution)/shard_map/dot_general | solution.py:96
  22.7 0.1 reshape.116
  22.8 6.6 %convolution_convert_fusion.1 = bf16[320,1024]{1,0:T(8,128)(2,1)} fusion(bf16[3584,1024]{1,0:T(8,128)(2,1)} %param.15, f32[3584]{0:T(1024)S(1)} %copy-done.10, f32[320]{0:T(512)S(1)} %add_sqrt_fusion.1, bf16[64,3584]{1,0:T(8,128)(2,1)S(1)} %copy-done, bf16[256,3584]{1,0:T(8,128)(2,1)S(1)} %copy-done.1), kind=kOutput, calls=%fused_computation.27 | convolution fusion | flops 2357166080 | bytes 10304768 | tf_op jit(solution)/shard_map/dot_general | solution.py:83
  29.4 2.5 reshape.112
  31.9 4.6 %convolution_convert_fusion.7 = bf16[64,1024]{1,0:T(8,128)(2,1)S(1)} fusion(bf16[3584,1024]{1,0:T(8,128)(2,1)} %param.15, bf16[64,3584]{1,0:T(8,128)(2,1)S(1)} %copy-done, f32[3584]{0:T(1024)S(1)} %copy-done.10, f32[64]{0:T(128)S(1)} %add_sqrt_fusion.7), kind=kOutput, calls=%fused_computation.50 | convolution fusion | flops 470745088 | bytes 7944448 | tf_op jit(solution)/shard_map/dot_general | solution.py:99
  36.4 0.1 reshape.115
  36.6 81.7 %all-gather.3.cloned.1.call-done = bf16[3584,2048]{1,0:T(8,128)(2,1)} async-done(((bf16[112,2048]{1,0:T(8,128)(2,1)}), bf16[3584,2048]{1,0:T(8,128)(2,1)}) %all-gather.3.cloned.1.call-update) | async-done | bytes 14680080 | tf_op jit(solution)/shard_map/all_gather | solution.py:77
  118.3 11.2 %fusion.6 = bf16[320,2048]{1,0:T(8,128)(2,1)} fusion(bf16[3584,2048]{1,0:T(8,128)(2,1)} %all-gather.3.cloned.1.call-done, f32[3584]{0:T(1024)S(1)} %copy-done.10, f32[320]{0:T(512)S(1)} %add_sqrt_fusion.1, bf16[64,3584]{1,0:T(8,128)(2,1)S(1)} %copy-done, bf16[256,3584]{1,0:T(8,128)(2,1)S(1)} %copy-done.1), kind=kOutput, calls=%fused_computation.12 | convolution fusion | flops 4706959360 | bytes 18300160 | tf_op jit(solution)/shard_map/dot_general | solution.py:75
  129.5 3.8 %reshape.114 = bf16[320,4,2,256]{3,2,1,0:T(2,128)(2,1)S(1)} reshape(bf16[320,2048]{1,0:T(8,128)(2,1)} %fusion.6) | data formatting | bytes 2621440 | tf_op jit(solution)/shard_map/reshape | solution.py:29
  133.3 1.2 slice.24
  134.4 0.2 reshape.117
  134.6 0.3 fusion.68
  134.9 1.3 fusion.4
  136.3 0.6 copy-done.9
  136.8 2.3 fusion.13
  139.1 0.3 fusion.22
  139.4 1.0 copy.35
  140.4 1.1 convert_element_type.117
  141.5 82.8 %all-gather.5.cloned.1.call-done = bf16[2048,3584]{1,0:T(8,128)(2,1)} async-done(((bf16[64,3584]{1,0:T(8,128)(2,1)}), bf16[2048,3584]{1,0:T(8,128)(2,1)}) %all-gather.5.cloned.1.call-update) | async-done | bytes 14680080 | tf_op jit(solution)/shard_map/all_gather | solution.py:80
  224.3 7.9 %multiply_reduce_fusion.2 = (f32[64]{0:T(128)S(1)}, f32[64,3584]{1,0:T(8,128)S(1)}) fusion(bf16[64,2048]{1,0:T(8,128)(2,1)S(1)} %convert_element_type.117, bf16[2048,3584]{1,0:T(8,128)(2,1)} %all-gather.5.cloned.1.call-done), kind=kOutput, calls=%fused_computation.75 | convolution fusion | flops 939982784 | bytes 15859968 | tf_op jit(solution)/shard_map/dot_general | solution.py:51
  232.2 0.2 fusion.41
  232.5 3.0 collective-permute-start
  235.4 0.8 collective-permute-done
  236.2 0.3 fusion.28
  236.5 0.5 copy-done.13
  237.0 5.2 %convolution_convert_fusion.5 = bf16[64,1024]{1,0:T(8,128)(2,1)} fusion(bf16[3584,1024]{1,0:T(8,128)(2,1)} %param.15, f32[64]{0:T(128)S(1)} %add_sqrt_fusion.5, f32[3584]{0:T(1024)} %param.11, bf16[64,3584]{1,0:T(8,128)(2,1)S(1)} %copy-done, bf16[64,3584]{1,0:T(8,128)(2,1)} %collective-permute-done, pred[]{:T(512)S(6)} %eq.3), kind=kOutput, calls=%fused_computation.48 | convolution fusion | flops 470974464 | bytes 8403201 | tf_op jit(solution)/shard_map/dot_general | solution.py:99
  242.2 1.6 reshape.118
  243.8 5.2 %convolution_convert_fusion.4 = bf16[64,1024]{1,0:T(8,128)(2,1)} fusion(bf16[3584,1024]{1,0:T(8,128)(2,1)} %param.14, f32[64]{0:T(128)} %copy-done.13, f32[3584]{0:T(1024)} %param.11, bf16[64,3584]{1,0:T(8,128)(2,1)S(1)} %copy-done, bf16[64,3584]{1,0:T(8,128)(2,1)} %collective-permute-done, pred[]{:T(512)S(6)} %eq.3), kind=kOutput, calls=%fused_computation.47 | convolution fusion | flops 470974464 | bytes 8403201 | tf_op jit(solution)/shard_map/dot_general | solution.py:96
  249.0 1.6 reshape.119
  250.7 1.3 fusion.69
  252.0 0.7 bitcast_add_fusion.2
  252.6 1.2 fusion.21
  253.8 1.0 copy.40
  254.8 1.8 convert_element_type.125
  256.6 8.0 %multiply_reduce_fusion.1 = (f32[64]{0:T(128)S(1)}, f32[64,3584]{1,0:T(8,128)S(1)}) fusion(bf16[64,2048]{1,0:T(8,128)(2,1)} %convert_element_type.125, bf16[2048,3584]{1,0:T(8,128)(2,1)} %all-gather.5.cloned.1.call-done), kind=kOutput, calls=%fused_computation.74 | convolution fusion | flops 939982784 | bytes 15859968 | tf_op jit(solution)/shard_map/dot_general | solution.py:51
  264.7 0.2 fusion.42
  264.9 0.8 copy-done.3
  265.7 8.7 %collective-permute-start.1 = (bf16[64,3584]{1,0:T(8,128)(2,1)S(1)}, bf16[64,3584]{1,0:T(8,128)(2,1)S(1)}, u32[]{:S(2)}, u32[]{:S(2)}) collective-permute-start(bf16[64,3584]{1,0:T(8,128)(2,1)S(1)} %fusion.42), channel_id=1, source_target_pairs={{0,1},{1,2},{2,3},{3,4},{4,5},{5,6},{6,7},{7,8},{8,9},{9,10},{10,1... | collective-permute-start | bytes 1376264 | tf_op jit(solution)/shard_map/ppermute | solution.py:17
  275.0 0.5 collective-permute-done.1
  275.5 0.3 fusion.31
  275.8 0.5 copy-done.6
  276.3 0.5 copy-done.12
  276.8 5.2 %convolution_convert_fusion.3 = bf16[64,1024]{1,0:T(8,128)(2,1)} fusion(bf16[3584,1024]{1,0:T(8,128)(2,1)} %param.15, f32[64]{0:T(128)S(1)} %add_sqrt_fusion.3, f32[3584]{0:T(1024)S(1)} %copy-done.11, bf16[64,3584]{1,0:T(8,128)(2,1)S(1)} %copy-done, bf16[64,3584]{1,0:T(8,128)(2,1)S(1)} %collective-permute-done.1, pred[]{:T(512)S(6)} %eq.3), kind=kOutput, calls=%fused_computation.46 | convolution fusion | flops 470974464 | bytes 8403201 | tf_op jit(solution)/shard_map/dot_general | solution.py:99
  282.0 1.6 reshape.120
  283.6 5.2 %convolution_convert_fusion.2 = bf16[64,1024]{1,0:T(8,128)(2,1)} fusion(bf16[3584,1024]{1,0:T(8,128)(2,1)} %param.14, f32[64]{0:T(128)} %copy-done.12, f32[3584]{0:T(1024)} %param.11, bf16[64,3584]{1,0:T(8,128)(2,1)S(1)} %copy-done, bf16[64,3584]{1,0:T(8,128)(2,1)} %copy-done.6, pred[]{:T(512)S(6)} %eq.3), kind=kOutput, calls=%fused_computation.45 | convolution fusion | flops 470974464 | bytes 8403201 | tf_op jit(solution)/shard_map/dot_general | solution.py:96
  288.8 1.6 reshape.121
  290.4 2.0 fusion.70
  292.4 0.7 bitcast_add_fusion.1
  293.2 1.5 fusion.8
  294.7 1.3 copy.44
  296.1 1.0 convert_element_type.133
  297.1 8.6 %multiply_reduce_fusion = (f32[320]{0:T(512)S(1)}, f32[320,3584]{1,0:T(8,128)S(1)}) fusion(bf16[320,2048]{1,0:T(8,128)(2,1)S(1)} %convert_element_type.133, bf16[2048,3584]{1,0:T(8,128)(2,1)} %all-gather.5.cloned.1.call-done), kind=kOutput, calls=%fused_computation.7 | convolution fusion | flops 4699913728 | bytes 20579584 | tf_op jit(solution)/shard_map/dot_general | solution.py:51
  305.7 1.0 fusion.3
  306.7 1.8 fusion.44
  310.5 0.1 pad_maximum_fusion.1
  310.6 1.3 slice.26
  311.9 49.8 %psum.7 = f32[3]{0:T(128)S(1)} all-reduce(f32[3]{0:T(128)S(1)} %pad_maximum_fusion.1), channel_id=1, replica_groups=mesh['seg'=32] {'seg'}, use_global_device_ids=true, to_apply=%region_14.15 | all-reduce | flops 3 | bytes 24 | tf_op jit(solution)/shard_map/psum | solution.py:122
  361.7 0.5 add_sqrt_fusion.2
  (34 shorter events, 0.3 us)
Async XLA Ops:
  7.2 111.1 %all-gather.3.cloned.1.call-start = ((), (), s32[]{:S(2)}) async-start(), calls=%async_computation | async-start | bytes 15138816 | tf_op jit(solution)/shard_map/all_gather | solution.py:77
  7.9 216.4 %all-gather.5.cloned.1.call-start = ((), (), s32[]{:S(2)}) async-start(), calls=%async_computation.1 | async-start | bytes 15138816 | tf_op jit(solution)/shard_map/all_gather | solution.py:80
  10.9 6.9 %copy-start = (bf16[64,3584]{1,0:T(8,128)(2,1)S(1)}, bf16[64,3584]{1,0:T(8,128)(2,1)}, u32[]{:S(2)}) copy-start(bf16[64,3584]{1,0:T(8,128)(2,1)} %param.10) | copy-start | bytes 1376260
  10.9 7.2 %copy-start.10 = (f32[3584]{0:T(1024)S(1)}, f32[3584]{0:T(1024)}, u32[]{:S(2)}) copy-start(f32[3584]{0:T(1024)} %param.11) | copy-start | bytes 43012
  18.0 4.8 %copy-start.1 = (bf16[256,3584]{1,0:T(8,128)(2,1)S(1)}, bf16[256,3584]{1,0:T(8,128)(2,1)}, u32[]{:S(2)}) copy-start(bf16[256,3584]{1,0:T(8,128)(2,1)} %param.9) | copy-start | bytes 5505028
  133.3 3.0 copy-start.5
  134.6 1.6 copy-start.7
  136.2 0.6 copy-start.9
  141.5 90.7 %copy-start.8 = (f32[3584]{0:T(1024)S(1)}, f32[3584]{0:T(1024)}, u32[]{:S(2)}) copy-start(f32[3584]{0:T(1024)} %param.12) | copy-start | bytes 43012
  232.5 3.7 %collective-permute-start = (bf16[64,3584]{1,0:T(8,128)(2,1)S(1)}, bf16[64,3584]{1,0:T(8,128)(2,1)}, u32[]{:S(2)}, u32[]{:S(2)}) collective-permute-start(bf16[64,3584]{1,0:T(8,128)(2,1)S(1)} %fusion.41), channel_id=1, source_target_pairs={{0,1},{1,2},{2,3},{3,4},{4,5},{5,6},{6,7},{7,8},{8,9},{9,10},{10,1... | collective-permute-start | bytes 1376264 | tf_op jit(solution)/shard_map/ppermute | solution.py:17
  236.4 0.5 copy-start.13
  256.6 20.1 %copy-start.11 = (f32[3584]{0:T(1024)S(1)}, f32[3584]{0:T(1024)}, u32[]{:S(2)}) copy-start(f32[3584]{0:T(1024)} %param.11) | copy-start | bytes 43012
  264.9 0.8 copy-start.3
  265.7 9.8 %collective-permute-start.1 = (bf16[64,3584]{1,0:T(8,128)(2,1)S(1)}, bf16[64,3584]{1,0:T(8,128)(2,1)S(1)}, u32[]{:S(2)}, u32[]{:S(2)}) collective-permute-start(bf16[64,3584]{1,0:T(8,128)(2,1)S(1)} %fusion.42), channel_id=1, source_target_pairs={{0,1},{1,2},{2,3},{3,4},{4,5},{5,6},{6,7},{7,8},{8,9},{9,10},{10,1... | collective-permute-start | bytes 1376264 | tf_op jit(solution)/shard_map/ppermute | solution.py:17
  275.5 0.8 copy-start.6
  276.2 0.5 copy-start.12
  297.1 8.6 %copy-start.2 = (bf16[256,3584]{1,0:T(8,128)(2,1)S(1)}, bf16[256,3584]{1,0:T(8,128)(2,1)}, u32[]{:S(2)}) copy-start(bf16[256,3584]{1,0:T(8,128)(2,1)} %param.9) | copy-start | bytes 5505028
  305.7 1.0 copy-start.4
Sparse Core Ops, SparseCore 0:
  10.8 107.4 all-gather.2
  121.2 103.0 all-gather.4
where the time goes:
time: 370 us; the launch traced here: 369 us
  waiting for transfers between devices  167 us (45%)
  matrix products  88.9 us (24%)
  blocking collectives  49.8 us (13%)
  local copies, waits for them, and re-layouts  26.3 us (7%)
  between operations  17 us (5%)
  starting transfers between devices  11.7 us (3%)
  other arithmetic  8.26 us (2%)
    all_gather x1, waiting for transfers between devices, shards(): output_full = lax.all_gather(output_weight, 'seg', axis=0, tiled=True)  82.8 us
    all_gather x1, waiting for transfers between devices, shards(): lax.all_gather(query_weight, 'seg', axis=0, tiled=True)  81.7 us
    psum x1, blocking collectives, shards(): totals = lax.psum(jnp.stack(squares), 'seg')  49.8 us
    dot_general x3, matrix products, finish(): proj = jnp.dot(attn, output_weight, preferred_element_type=jnp.float32)  24.5 us
    dot_general x3, matrix products, shards(): jnp.dot(read_norm, key_matrix, preferred_element_type=jnp.float32)  15.1 us
    dot_general x3, matrix products, shards(): jnp.dot(read_norm, value_matrix, preferred_element_type=jnp.float32)  15 us
    ppermute x2, starting transfers between devices, from_behind(): return lax.ppermute(block, axis, route)  11.6 us
    dot_general x1, matrix products, shards(): jnp.dot(normed, lax.all_gather(query_weight, 'seg', axis=0, tiled=True),...  11.2 us
  transfers between devices with their start and end apart: 4, of which 4 were waited for; matrix products, arithmetic and copies ran while one was open for 14% of the time, Pallas kernels for 0%

commit v1 on v0

v1 whole, which is shorter than its diff:
```python
import functools

import jax
import jax.numpy as jnp
from jax import lax
from jax.experimental import pallas as pl
from jax.experimental.pallas import tpu as pltpu
from jax.sharding import PartitionSpec as P


HEAD_WIDTH = 256
KEY_VALUE_HEADS = 4
ITERS = 3
LANES = 128
MESH = pl.DeviceIdType.MESH


eps = 1e-06


def from_behind(block, axis, distance):
    devices = range(lax.axis_size(axis))
    route = [(i - distance, i) for i in devices if i - distance in devices]
    return lax.ppermute(block, axis, route)


def prenorm(rows, gain):
    rows = rows.astype(jnp.float32)
    mean_sq = jnp.mean(rows * rows, axis=-1, keepdims=True)
    return (rows / jnp.sqrt(mean_sq + eps) * gain).astype(jnp.bfloat16)


def reduce_kernel(n, part_ref, out_ref, held, total, send1, recv1, send2, recv2):
    me = lax.axis_index("seg")

    def scatter(k):
        to = lax.rem(me + k, n)
        return pltpu.make_async_remote_copy(
            src_ref=part_ref.at[to],
            dst_ref=held.at[k],
            send_sem=send1.at[k],
            recv_sem=recv1.at[k],
            device_id=(to,),
            device_id_type=MESH,
        )

    def spread(k):
        to = lax.rem(me + k, n)
        return pltpu.make_async_remote_copy(
            src_ref=total,
            dst_ref=out_ref.at[me],
            send_sem=send2.at[k],
            recv_sem=recv2.at[k],
            device_id=(to,),
            device_id_type=MESH,
        )

    @pl.loop(1, n)
    def _(k):
        scatter(k).start()

    total[...] = part_ref[me]

    @pl.loop(1, n)
    def _(k):
        scatter(k).wait_recv()
        total[...] += held[k]

    @pl.loop(1, n)
    def _(k):
        spread(k).start()

    out_ref[me] = total[...]

    @pl.loop(1, n)
    def _(k):
        scatter(k).wait_send()
        spread(k).wait()


def all_sum(parts):
    n = parts.shape[0]
    sems = pltpu.SemaphoreType.DMA((n,))
    return pl.pallas_call(
        functools.partial(reduce_kernel, n),
        out_shape=jax.ShapeDtypeStruct(parts.shape, parts.dtype),
        in_specs=[pl.BlockSpec(memory_space=pltpu.VMEM)],
        out_specs=pl.BlockSpec(memory_space=pltpu.VMEM),
        scratch_shapes=[
            pltpu.VMEM(parts.shape, parts.dtype),
            pltpu.VMEM(parts.shape[1:], parts.dtype),
            sems,
            sems,
            sems,
            sems,
        ],
        compiler_params=pltpu.CompilerParams(has_side_effects=True),
        cost_estimate=pl.CostEstimate(flops=0, bytes_accessed=30_000_000, transcendentals=0),
        name="query_sum",
    )(parts)


def total_kernel(n, part_ref, out_ref, held, send, recv):
    me = lax.axis_index("seg")

    def copy(k):
        return pltpu.make_async_remote_copy(
            src_ref=part_ref,
            dst_ref=held.at[me],
            send_sem=send.at[k],
            recv_sem=recv.at[k],
            device_id=(lax.rem(me + k, n),),
            device_id_type=MESH,
        )

    @pl.loop(1, n)
    def _(k):
        copy(k).start()

    held[me] = part_ref[...]

    @pl.loop(1, n)
    def _(k):
        copy(k).wait()

    out_ref[...] = jnp.sum(held[...], axis=0)


def small_sum(part, n):
    sems = pltpu.SemaphoreType.DMA((n,))
    return pl.pallas_call(
        functools.partial(total_kernel, n),
        out_shape=jax.ShapeDtypeStruct(part.shape, part.dtype),
        in_specs=[pl.BlockSpec(memory_space=pltpu.VMEM)],
        out_specs=pl.BlockSpec(memory_space=pltpu.VMEM),
        scratch_shapes=[pltpu.VMEM((n,) + part.shape, part.dtype), sems, sems],
        compiler_params=pltpu.CompilerParams(has_side_effects=True),
        cost_estimate=pl.CostEstimate(flops=0, bytes_accessed=8_000_000, transcendentals=0),
        name="change_sum",
    )(part)


def attend_kernel(first, keys, q_ref, rk_ref, rv_ref, k_ref, v_ref, out_ref):
    rows = q_ref.shape[0]
    nt = (((1,), (1,)), ((), ()))
    row = lax.broadcasted_iota(jnp.int32, (rows, keys), 0)
    col = lax.broadcasted_iota(jnp.int32, (rows, keys), 1)
    allowed = col <= row + first
    for half in range(2):
        cols = slice(half * HEAD_WIDTH, (half + 1) * HEAD_WIDTH)
        q = q_ref[:, cols]
        own = lax.dot_general(q, k_ref[:keys], nt, preferred_element_type=jnp.float32)
        own = jnp.where(allowed, jnp.exp(own), 0.0)
        read = jnp.exp(
            lax.dot_general(q, rk_ref[...], nt, preferred_element_type=jnp.float32)
        )
        denom = jnp.sum(own, axis=-1, keepdims=True) + jnp.sum(read, axis=-1, keepdims=True)
        numer = jnp.dot(
            own.astype(jnp.bfloat16), v_ref[:keys], preferred_element_type=jnp.float32
        ) + jnp.dot(read.astype(jnp.bfloat16), rv_ref[...], preferred_element_type=jnp.float32)
        out_ref[:, cols] = (numer / denom).astype(jnp.bfloat16)


def attend(q, read_k, read_v, local_k, local_v, first, keys):
    rows, width = q.shape
    mem, total = read_k.shape[0], local_k.shape[0]
    at = lambda h: (0, h)
    return pl.pallas_call(
        functools.partial(attend_kernel, first, keys),
        grid=(KEY_VALUE_HEADS,),
        out_shape=jax.ShapeDtypeStruct((rows, width), jnp.bfloat16),
        in_specs=[
            pl.BlockSpec((rows, 2 * HEAD_WIDTH), at),
            pl.BlockSpec((mem, HEAD_WIDTH), at),
            pl.BlockSpec((mem, HEAD_WIDTH), at),
            pl.BlockSpec((total, HEAD_WIDTH), at),
            pl.BlockSpec((total, HEAD_WIDTH), at),
        ],
        out_specs=pl.BlockSpec((rows, 2 * HEAD_WIDTH), at),
        cost_estimate=pl.CostEstimate(
            flops=4 * rows * width * (keys + mem), bytes_accessed=6_000_000, transcendentals=0
        ),
        name="attend",
    )(q, read_k, read_v, local_k, local_v)


def finish(inputs, attn, output_weight, post_gain):
    proj = jnp.dot(attn, output_weight, preferred_element_type=jnp.float32)
    mean_sq = jnp.mean(proj * proj, axis=-1, keepdims=True)
    return (inputs.astype(jnp.float32) + proj / jnp.sqrt(mean_sq + eps) * post_gain).astype(
        jnp.bfloat16
    )


def shards(
    tokens,
    memory,
    norm_gain,
    post_gain,
    query_weight,
    key_matrix,
    value_matrix,
    output_weight,
    segment_weight,
):
    n = lax.axis_size("seg")
    me = lax.axis_index("seg")
    tok_rows = tokens.shape[0]
    mem_rows, feature_width = memory.shape
    own_rows, query_width = query_weight.shape
    scale = 1.0 / HEAD_WIDTH**0.5
    output_full = lax.all_gather(output_weight, "seg", axis=0, tiled=True)

    mem_norm = prenorm(memory, norm_gain)
    own_cols = lax.dynamic_slice_in_dim(mem_norm, me * own_rows, own_rows, axis=1)
    part = jnp.dot(own_cols, query_weight, preferred_element_type=jnp.float32)
    blocks = query_width // LANES
    part = jnp.transpose(part.reshape(mem_rows, blocks, LANES), (1, 0, 2))
    summed = all_sum(part.reshape(n, mem_rows * blocks // n, LANES))
    summed = jnp.transpose(summed.reshape(blocks, mem_rows, LANES), (1, 0, 2))
    write_q = (summed.reshape(mem_rows, query_width) * scale).astype(jnp.bfloat16)

    own_query, write_q = lax.optimization_barrier((query_weight, write_q))
    query_full = lax.all_gather(own_query, "seg", axis=0, tiled=True)

    normed = prenorm(jnp.concatenate([tokens, memory], axis=0), norm_gain)
    local_k = jnp.dot(normed, key_matrix, preferred_element_type=jnp.float32).astype(jnp.bfloat16)
    local_v = jnp.dot(normed, value_matrix, preferred_element_type=jnp.float32).astype(jnp.bfloat16)
    total_rows = tok_rows + mem_rows
    first = jnp.int32(0) == me
    previous = memory
    squares = []
    own_weight = segment_weight[0]
    count_all = n * mem_rows * feature_width
    read_k, read_v = local_k[tok_rows:], local_v[tok_rows:]
    for step in range(ITERS):
        attn = attend(write_q, read_k, read_v, local_k, local_v, tok_rows, total_rows)
        newest = finish(memory, attn, output_full, post_gain)
        diff = newest.astype(jnp.float32) - previous.astype(jnp.float32)
        squares.append(jnp.sum(diff * diff) * own_weight)
        previous = newest
        if step + 1 < ITERS:
            read = jnp.where(first, memory, from_behind(newest, "seg", 1))
            read_norm = prenorm(read, norm_gain)
            read_k = jnp.dot(read_norm, key_matrix, preferred_element_type=jnp.float32).astype(
                jnp.bfloat16
            )
            read_v = jnp.dot(read_norm, value_matrix, preferred_element_type=jnp.float32).astype(
                jnp.bfloat16
            )
    squares = jnp.broadcast_to(jnp.pad(jnp.stack(squares), (0, LANES - ITERS))[None], (8, LANES))
    totals = small_sum(squares, n)[0, :ITERS]
    change_vec = jnp.sqrt(totals / count_all + eps)

    query_acc = jnp.dot(normed[:tok_rows], query_full, preferred_element_type=jnp.float32)
    query_vectors = (query_acc * scale).astype(jnp.bfloat16)
    attn = attend(query_vectors, read_k, read_v, local_k, local_v, 0, tok_rows)
    token_out = finish(tokens, attn, output_full, post_gain)
    return (token_out, previous, change_vec)


def solution(mesh):
    return jax.shard_map(
        shards,
        mesh=mesh,
        in_specs=(
            P("seg", None),
            P(),
            P(),
            P(),
            P("seg", None),
            P(),
            P(),
            P("seg", None),
            P("seg"),
        ),
        out_specs=(P("seg", None), P("seg", None), P()),
        check_vma=False,
    )
```

time: 370 us -> 318 us (0.86)
  Pallas kernels: 0 us -> 77.3 us
  blocking collectives: 49.8 us -> 0 us
  waiting for transfers between devices: 167 us -> 121 us
  local copies, waits for them, and re-layouts: 26.3 us -> 4.86 us
  matrix products: 88.9 us -> 70.2 us
  other arithmetic: 8.26 us -> 15.2 us
    pallas_call x0 -> x6, Pallas kernels: none -> 77.3 us  [the longest x1 46.5 us: all_sum(): pl.pallas_call(functools.partial(reduce_kernel, n), out_shape=jax.ShapeDt...]
    psum x1 -> x0, blocking collectives: 49.8 us -> none  [shards(): totals = lax.psum(jnp.stack(squares), 'seg')]
    all_gather x1, waiting for transfers between devices: 82.8 us -> 55.2 us  [shards(): output_full = lax.all_gather(output_weight, 'seg', axis=0, tiled=True)]
    all_gather x1, waiting for transfers between devices: 81.7 us -> 64.2 us  [shards(): query_full = lax.all_gather(own_query, 'seg', axis=0, tiled=True)]
    reshape x10 -> x1, local copies, waits for them, and re-layouts: 13.6 us -> 0.85 us  [shards(): part = jnp.transpose(part.reshape(mem_rows, blocks, LANES), (1, 0, 2))]
    dot_general x9 -> x2, matrix products: 21.3 us -> 9.81 us  [the longest x1 8.51 us: shards(): jnp.dot(normed[:tok_rows], query_full, preferred_element_type=jnp.float32)]
    convert_element_type x6 -> x1, local copies, waits for them, and re-layouts: 7.26 us -> 0.18 us  [shards(): (summed.reshape(mem_rows, query_width) * scale).astype(jnp.bfloat16)]
    dot_general x3 -> x4, matrix products: 24.5 us -> 30.2 us  [finish(): proj = jnp.dot(attn, output_weight, preferred_element_type=jnp.float32)]
  transfers between devices with their start and end apart: 4 -> 4, of which waited for: 4 -> 3; matrix products, arithmetic and copies ran while one was open for 14% -> 18% of each run, Pallas kernels for 0% -> 17%
where the time goes in v1:
time: 318 us; the launch traced here: 317 us
  waiting for transfers between devices  121 us (38%)
  Pallas kernels  77.3 us (24%)
  matrix products  70.2 us (22%)
  between operations  16.9 us (5%)
  other arithmetic  15.2 us (5%)
  starting transfers between devices  12.3 us (4%)
  local copies, waits for them, and re-layouts  4.86 us (2%)
    all_gather x1, waiting for transfers between devices, shards(): query_full = lax.all_gather(own_query, 'seg', axis=0, tiled=True)  64.2 us
    all_gather x1, waiting for transfers between devices, shards(): output_full = lax.all_gather(output_weight, 'seg', axis=0, tiled=True)  55.2 us
    pallas_call x1, Pallas kernels, all_sum(): pl.pallas_call(functools.partial(reduce_kernel, n), out_shape=jax.ShapeDt...  46.5 us
    dot_general x4, matrix products, finish(): proj = jnp.dot(attn, output_weight, preferred_element_type=jnp.float32)  30.2 us
    pallas_call x4, Pallas kernels, attend(): pl.pallas_call(functools.partial(attend_kernel, first, keys), grid=(KEY_V...  18.4 us
    pallas_call x1, Pallas kernels, small_sum(): pl.pallas_call(functools.partial(total_kernel, n), out_shape=jax.ShapeDty...  12.4 us
    ppermute x2, starting transfers between devices, from_behind(): return lax.ppermute(block, axis, route)  12.2 us
    dot_general x2, matrix products, shards(): jnp.dot(read_norm, key_matrix, preferred_element_type=jnp.float32)  10.4 us
  transfers between devices with their start and end apart: 4, of which 3 were waited for; matrix products, arithmetic and copies ran while one was open for 18% of the time, Pallas kernels for 17%

profile of v1, /device:TPU:0, one launch (start us, length us, event | category | flops | bytes accessed | tf_op | source)
XLA Modules:
  0.0 317.4 jit_solution(2894028506992075635)
XLA Ops:
  7.2 0.0 copy-start
  7.2 0.0 copy-start.1
  7.2 0.0 all-gather.5.cloned.1.call-start
  7.2 0.7 all-gather.5.cloned.1.call-update
  7.9 0.0 all-gather.3.cloned.1.call-start
  8.0 0.0 copy-start.8
  8.0 1.1 convert_element_type.92
  9.1 0.8 dynamic-slice
  9.9 1.2 fusion.15
  11.1 1.3 convolution_bitcast_fusion
  12.4 0.9 copy.18
  13.2 46.5 %query_sum.1 = f32[32,32,128]{2,1,0:T(8,128)} custom-call(f32[32,32,128]{2,1,0:T(8,128)} %bitcast.46), custom_call_target="tpu_custom_call" | custom-call | bytes 30000000 | tf_op jit(solution)/shard_map/query_sum/pallas_call | solution.py:84
  59.7 1.1 multiply_convert_fusion
  60.8 0.2 copy.13
  61.0 0.8 copy.19
  61.8 0.0 all-gather.3.cloned.1.call-update
  61.8 0.0 copy-done
  61.8 0.0 copy-done.1
  61.8 0.5 fusion
  62.4 0.0 copy-done.8
  62.4 0.0 slice-start.4
  62.4 0.7 fusion.2
  63.1 0.0 copy-start.4
  63.1 0.0 slice-start.5
  63.2 6.8 %convolution_convert_fusion.1.k_ref = bf16[320,1024]{1,0:T(8,128)(2,1)S(1)} fusion(bf16[320,3584]{1,0:T(8,128)(2,1)S(1)} %fusion.2, bf16[3584,1024]{1,0:T(8,128)(2,1)} %param.14), kind=kOutput, calls=%fused_computation.12 | convolution fusion | flops 2349137920 | bytes 10289152 | tf_op jit(solution)/shard_map/dot_general | solution.py:227
  70.0 0.0 copy-start.2
  70.0 0.7 slice.17.rk_ref
  70.7 0.0 copy-done.4
  70.7 0.0 slice-done.4
  70.7 0.0 slice-done.5
  70.7 2.5 convolution_convert_fusion.v_ref
  73.3 0.0 copy-done.2
  73.3 0.7 slice.18.rv_ref
  74.0 0.2 copy-done.3
  74.2 4.5 %attend.4 = bf16[64,2048]{1,0:T(8,128)(2,1)} custom-call(bf16[64,2048]{1,0:T(8,128)(2,1)} %bitcast.43, bf16[64,1024]{1,0:T(8,128)(2,1)} %slice.17.rk_ref, bf16[64,1024]{1,0:T(8,128)(2,1)} %slice.18.rv_ref, bf16[320,1024]{1,0:T(8,128)(2,1)} %copy-done.2, bf16[320,1024]{1,0:T(8,128)(2,1)} %copy-done.3), custom_call_target="tpu_custom_call" | custom-call | flops 201326592 | bytes 6000000 | tf_op jit(solution)/shard_map/attend/pallas_call | solution.py:168
  78.6 55.2 %all-gather.5.cloned.1.call-done = bf16[2048,3584]{1,0:T(8,128)(2,1)} async-done(((bf16[64,3584]{1,0:T(8,128)(2,1)}), bf16[2048,3584]{1,0:T(8,128)(2,1)}) %all-gather.5.cloned.1.call-update) | async-done | bytes 14680080 | tf_op jit(solution)/shard_map/all_gather | solution.py:212
  133.9 8.0 %multiply_reduce_fusion.3 = (f32[64]{0:T(128)S(1)}, f32[64,3584]{1,0:T(8,128)S(1)}) fusion(bf16[64,2048]{1,0:T(8,128)(2,1)} %attend.4, bf16[2048,3584]{1,0:T(8,128)(2,1)} %all-gather.5.cloned.1.call-done), kind=kOutput, calls=%fused_computation.47 | convolution fusion | flops 939982784 | bytes 15859968 | tf_op jit(solution)/shard_map/dot_general | solution.py:188
  141.9 0.2 fusion.16
  142.1 2.4 collective-permute-start
  145.1 0.6 collective-permute-done
  145.7 0.2 fusion.5
  146.0 5.2 %convolution_convert_fusion.5.rk_ref = bf16[64,1024]{1,0:T(8,128)(2,1)} fusion(bf16[3584,1024]{1,0:T(8,128)(2,1)} %param.14, f32[64]{0:T(128)S(1)} %add_sqrt_fusion.5, f32[3584]{0:T(1024)S(1)} %copy-done.8, bf16[64,3584]{1,0:T(8,128)(2,1)S(1)} %copy-done, bf16[64,3584]{1,0:T(8,128)(2,1)S(1)} %collective-permute-done, pred[]{:T(512)S(6)} %eq.3), kind=kOutput, calls=%fused_computation.17 | convolution fusion | flops 470974464 | bytes 8403201 | tf_op jit(solution)/shard_map/dot_general | solution.py:245
  151.2 5.2 %convolution_convert_fusion.4.rv_ref = bf16[64,1024]{1,0:T(8,128)(2,1)} fusion(bf16[3584,1024]{1,0:T(8,128)(2,1)} %param.15, f32[64]{0:T(128)S(1)} %add_sqrt_fusion.5, f32[3584]{0:T(1024)S(1)} %copy-done.8, bf16[64,3584]{1,0:T(8,128)(2,1)S(1)} %copy-done, bf16[64,3584]{1,0:T(8,128)(2,1)S(1)} %collective-permute-done, pred[]{:T(512)S(6)} %eq.3), kind=kOutput, calls=%fused_computation.16 | convolution fusion | flops 470974464 | bytes 8403201 | tf_op jit(solution)/shard_map/dot_general | solution.py:248
  156.4 4.5 %attend.5 = bf16[64,2048]{1,0:T(8,128)(2,1)} custom-call(bf16[64,2048]{1,0:T(8,128)(2,1)} %bitcast.44, bf16[64,1024]{1,0:T(8,128)(2,1)} %convolution_convert_fusion.5.rk_ref, bf16[64,1024]{1,0:T(8,128)(2,1)} %convolution_convert_fusion.4.rv_ref, bf16[320,1024]{1,0:T(8,128)(2,1)} %copy-done.2, bf16[320,1024]{1,0:T(8,128)(2,1)} %copy-done.3), custom_call_target="tpu_custom_call" | custom-call | flops 201326592 | bytes 6000000 | tf_op jit(solution)/shard_map/attend/pallas_call | solution.py:168
  160.8 8.1 %multiply_reduce_fusion.2 = (f32[64]{0:T(128)S(1)}, f32[64,3584]{1,0:T(8,128)S(1)}) fusion(bf16[64,2048]{1,0:T(8,128)(2,1)} %attend.5, bf16[2048,3584]{1,0:T(8,128)(2,1)} %all-gather.5.cloned.1.call-done), kind=kOutput, calls=%fused_computation.46 | convolution fusion | flops 939982784 | bytes 15859968 | tf_op jit(solution)/shard_map/dot_general | solution.py:188
  169.0 1.0 fusion.17
  170.0 9.9 %collective-permute-start.1 = (bf16[64,3584]{1,0:T(8,128)(2,1)}, bf16[64,3584]{1,0:T(8,128)(2,1)}, u32[]{:S(2)}, u32[]{:S(2)}) collective-permute-start(bf16[64,3584]{1,0:T(8,128)(2,1)} %fusion.17), channel_id=1, source_target_pairs={{0,1},{1,2},{2,3},{3,4},{4,5},{5,6},{6,7},{7,8},{8,9},{9,10},{10,1... | collective-permute-start | bytes 1376264 | tf_op jit(solution)/shard_map/ppermute | solution.py:24
  179.9 64.2 %all-gather.3.cloned.1.call-done = bf16[3584,2048]{1,0:T(8,128)(2,1)} async-done(((bf16[112,2048]{1,0:T(8,128)(2,1)}), bf16[3584,2048]{1,0:T(8,128)(2,1)}) %all-gather.3.cloned.1.call-update) | async-done | bytes 14680080 | tf_op jit(solution)/shard_map/all_gather | solution.py:224
  244.1 8.5 %fusion.3.q_ref = bf16[256,2048]{1,0:T(8,128)(2,1)} fusion(bf16[3584,2048]{1,0:T(8,128)(2,1)} %all-gather.3.cloned.1.call-done, bf16[320,3584]{1,0:T(8,128)(2,1)S(1)} %copy-done.5), kind=kOutput, calls=%fused_computation.8 | convolution fusion | flops 3759144960 | bytes 17563648 | tf_op jit(solution)/shard_map/dot_general | solution.py:255
  252.6 0.0 collective-permute-done.1
  252.6 0.3 fusion.8
  252.9 5.2 %convolution_convert_fusion.3.rk_ref = bf16[64,1024]{1,0:T(8,128)(2,1)} fusion(bf16[3584,1024]{1,0:T(8,128)(2,1)} %param.14, f32[64]{0:T(128)S(1)} %add_sqrt_fusion.3, f32[3584]{0:T(1024)S(1)} %copy-done.8, bf16[64,3584]{1,0:T(8,128)(2,1)S(1)} %copy-done, bf16[64,3584]{1,0:T(8,128)(2,1)} %collective-permute-done.1, pred[]{:T(512)S(6)} %eq.3), kind=kOutput, calls=%fused_computation.15 | convolution fusion | flops 470974464 | bytes 8403201 | tf_op jit(solution)/shard_map/dot_general | solution.py:245
  258.1 5.2 %convolution_convert_fusion.2.rv_ref = bf16[64,1024]{1,0:T(8,128)(2,1)} fusion(bf16[3584,1024]{1,0:T(8,128)(2,1)} %param.15, f32[64]{0:T(128)S(1)} %add_sqrt_fusion.3, f32[3584]{0:T(1024)S(1)} %copy-done.8, bf16[64,3584]{1,0:T(8,128)(2,1)S(1)} %copy-done, bf16[64,3584]{1,0:T(8,128)(2,1)} %collective-permute-done.1, pred[]{:T(512)S(6)} %eq.3), kind=kOutput, calls=%fused_computation.14 | convolution fusion | flops 470974464 | bytes 8403201 | tf_op jit(solution)/shard_map/dot_general | solution.py:248
  263.3 4.5 %attend.7 = bf16[64,2048]{1,0:T(8,128)(2,1)} custom-call(bf16[64,2048]{1,0:T(8,128)(2,1)} %bitcast.45, bf16[64,1024]{1,0:T(8,128)(2,1)} %convolution_convert_fusion.3.rk_ref, bf16[64,1024]{1,0:T(8,128)(2,1)} %convolution_convert_fusion.2.rv_ref, bf16[320,1024]{1,0:T(8,128)(2,1)} %copy-done.2, bf16[320,1024]{1,0:T(8,128)(2,1)} %copy-done.3), custom_call_target="tpu_custom_call" | custom-call | flops 201326592 | bytes 6000000 | tf_op jit(solution)/shard_map/attend/pallas_call | solution.py:168
  267.7 5.0 %attend.6 = bf16[256,2048]{1,0:T(8,128)(2,1)} custom-call(bf16[256,2048]{1,0:T(8,128)(2,1)} %fusion.3.q_ref, bf16[64,1024]{1,0:T(8,128)(2,1)} %convolution_convert_fusion.3.rk_ref, bf16[64,1024]{1,0:T(8,128)(2,1)} %convolution_convert_fusion.2.rv_ref, bf16[320,1024]{1,0:T(8,128)(2,1)} %copy-done.2, bf16[320,1024]{1,0:T(8,128)(2,1)} %copy-done.3), custom_call_target="tpu_custom_call" | custom-call | flops 671088640 | bytes 6000000 | tf_op jit(solution)/shard_map/attend/pallas_call | solution.py:168
  272.7 0.0 copy-start.6
  272.7 11.4 %multiply_reduce_fusion = (f32[256]{0:T(256)S(1)}, f32[256,3584]{1,0:T(8,128)}) fusion(bf16[256,2048]{1,0:T(8,128)(2,1)} %attend.6, bf16[2048,3584]{1,0:T(8,128)(2,1)} %all-gather.5.cloned.1.call-done), kind=kOutput, calls=%fused_computation.6 | convolution fusion | flops 3759931136 | bytes 19399680 | tf_op jit(solution)/shard_map/dot_general | solution.py:188
  284.1 2.7 multiply_reduce_fusion.1
  286.9 3.0 fusion.20
  291.8 0.1 select_maximum_fusion
  291.9 0.6 broadcast_in_dim.2.part_ref
  292.5 12.4 %change_sum.1 = f32[8,128]{1,0:T(8,128)} custom-call(f32[8,128]{1,0:T(8,128)} %broadcast_in_dim.2.part_ref), custom_call_target="tpu_custom_call" | custom-call | bytes 8000000 | tf_op jit(solution)/shard_map/change_sum/pallas_call | solution.py:131
  304.9 1.2 sqrt_bitcast_fusion
  306.1 4.5 %add_convert_fusion = bf16[256,3584]{1,0:T(8,128)(2,1)} fusion(f32[256,3584]{1,0:T(8,128)} %get-tuple-element.16, bf16[256,3584]{1,0:T(8,128)(2,1)} %param.9, f32[3584]{0:T(1024)S(1)} %copy-done.7, f32[256]{0:T(256)S(1)} %add_sqrt_fusion.1), kind=kLoop, calls=%fused_computation.5 | loop fusion | flops 4587520 | bytes 7355392 | tf_op jit(solution)/shard_map/convert_element_type | solution.py:190
  (24 shorter events, 0.1 us)
Async XLA Ops:
  7.2 54.7 %copy-start = (bf16[64,3584]{1,0:T(8,128)(2,1)S(1)}, bf16[64,3584]{1,0:T(8,128)(2,1)}, u32[]{:S(2)}) copy-start(bf16[64,3584]{1,0:T(8,128)(2,1)} %param.10) | copy-start | bytes 1376260
  7.2 54.7 %copy-start.1 = (bf16[256,3584]{1,0:T(8,128)(2,1)S(1)}, bf16[256,3584]{1,0:T(8,128)(2,1)}, u32[]{:S(2)}) copy-start(bf16[256,3584]{1,0:T(8,128)(2,1)} %param.9) | copy-start | bytes 5505028
  7.2 126.7 %all-gather.5.cloned.1.call-start = ((), (), s32[]{:S(2)}) async-start(), calls=%async_computation.1 | async-start | bytes 15138816 | tf_op jit(solution)/shard_map/all_gather | solution.py:212
  7.9 236.2 %all-gather.3.cloned.1.call-start = ((), (), s32[]{:S(2)}) async-start(), calls=%async_computation | async-start | bytes 15138816 | tf_op jit(solution)/shard_map/all_gather | solution.py:224
  8.0 54.4 %copy-start.8 = (f32[3584]{0:T(1024)S(1)}, f32[3584]{0:T(1024)}, u32[]{:S(2)}) copy-start(f32[3584]{0:T(1024)} %param.11) | copy-start | bytes 43012
  62.4 8.3 %slice-start.4 = ((s8[7340032]{0:T(1024)(128)(4,1)}), s8[4194304]{0:T(1024)(128)(4,1)S(1)}, s32[]{:S(2)}) async-start(s8[7340032]{0:T(1024)(128)(4,1)} %bitcast.49), calls=%async_computation.6 | async-start | bytes 8388608
  63.1 7.6 %copy-start.4 = (bf16[320,3584]{1,0:T(8,128)(2,1)}, bf16[320,3584]{1,0:T(8,128)(2,1)S(1)}, u32[]{:S(2)}) copy-start(bf16[320,3584]{1,0:T(8,128)(2,1)S(1)} %fusion.2) | copy-start | bytes 6881284
  63.1 7.6 %slice-start.5 = ((s8[7340032]{0:T(1024)(128)(4,1)}), s8[3145728]{0:T(1024)(128)(4,1)S(1)}, s32[]{:S(2)}) async-start(s8[7340032]{0:T(1024)(128)(4,1)} %bitcast.49), calls=%async_computation.7 | async-start | bytes 6291456
  70.0 3.3 %copy-start.2 = (bf16[320,1024]{1,0:T(8,128)(2,1)}, bf16[320,1024]{1,0:T(8,128)(2,1)S(1)}, u32[]{:S(2)}) copy-start(bf16[320,1024]{1,0:T(8,128)(2,1)S(1)} %convolution_convert_fusion.1.k_ref) | copy-start | bytes 1966084
  73.3 0.9 copy-start.3
  78.6 63.2 %copy-start.7 = (f32[3584]{0:T(1024)S(1)}, f32[3584]{0:T(1024)}, u32[]{:S(2)}) copy-start(f32[3584]{0:T(1024)} %param.12) | copy-start | bytes 43012
  142.1 3.6 %collective-permute-start = (bf16[64,3584]{1,0:T(8,128)(2,1)S(1)}, bf16[64,3584]{1,0:T(8,128)(2,1)S(1)}, u32[]{:S(2)}, u32[]{:S(2)}) collective-permute-start(bf16[64,3584]{1,0:T(8,128)(2,1)S(1)} %fusion.16), channel_id=1, source_target_pairs={{0,1},{1,2},{2,3},{3,4},{4,5},{5,6},{6,7},{7,8},{8,9},{9,10},{10,1... | collective-permute-start | bytes 1376264 | tf_op jit(solution)/shard_map/ppermute | solution.py:24
  160.8 83.2 %copy-start.5 = (bf16[320,3584]{1,0:T(8,128)(2,1)S(1)}, bf16[320,3584]{1,0:T(8,128)(2,1)}, u32[]{:S(2)}) copy-start(bf16[320,3584]{1,0:T(8,128)(2,1)} %copy-done.4) | copy-start | bytes 6881284
  170.0 82.6 %collective-permute-start.1 = (bf16[64,3584]{1,0:T(8,128)(2,1)}, bf16[64,3584]{1,0:T(8,128)(2,1)}, u32[]{:S(2)}, u32[]{:S(2)}) collective-permute-start(bf16[64,3584]{1,0:T(8,128)(2,1)} %fusion.17), channel_id=1, source_target_pairs={{0,1},{1,2},{2,3},{3,4},{4,5},{5,6},{6,7},{7,8},{8,9},{9,10},{10,1... | collective-permute-start | bytes 1376264 | tf_op jit(solution)/shard_map/ppermute | solution.py:24
  267.7 16.4 %slice-start = ((s8[14680064]{0:T(1024)(128)(4,1)}), s8[2097152]{0:T(1024)(128)(4,1)S(1)}, s32[]{:S(2)}) async-start(s8[14680064]{0:T(1024)(128)(4,1)} %bitcast.41), calls=%async_computation.2 | async-start | bytes 4194304
  272.7 11.4 %slice-start.1 = ((s8[14680064]{0:T(1024)(128)(4,1)}), s8[4194304]{0:T(1024)(128)(4,1)S(1)}, s32[]{:S(2)}) async-start(s8[14680064]{0:T(1024)(128)(4,1)} %bitcast.41), calls=%async_computation.3 | async-start | bytes 8388608
  272.7 11.4 %slice-start.2 = ((s8[14680064]{0:T(1024)(128)(4,1)}), s8[4194304]{0:T(1024)(128)(4,1)S(1)}, s32[]{:S(2)}) async-start(s8[14680064]{0:T(1024)(128)(4,1)} %bitcast.41), calls=%async_computation.4 | async-start | bytes 8388608
  272.7 11.4 %slice-start.3 = ((s8[14680064]{0:T(1024)(128)(4,1)}), s8[4194304]{0:T(1024)(128)(4,1)S(1)}, s32[]{:S(2)}) async-start(s8[14680064]{0:T(1024)(128)(4,1)} %bitcast.41), calls=%async_computation.5 | async-start | bytes 8388608
  272.7 11.4 %copy-start.6 = (bf16[64,2048]{1,0:T(8,128)(2,1)S(1)}, bf16[64,2048]{1,0:T(8,128)(2,1)}, u32[]{:S(2)}) copy-start(bf16[64,2048]{1,0:T(8,128)(2,1)} %attend.7) | copy-start | bytes 786436
Sparse Core Ops, SparseCore 0:
  10.9 122.9 all-gather.4
  136.7 107.3 all-gather.2

commit v2 on v1

--- a/solution.py
+++ b/solution.py
@@ -30,8 +30,9 @@
     return (rows / jnp.sqrt(mean_sq + eps) * gain).astype(jnp.bfloat16)
 
 
-def reduce_kernel(n, part_ref, out_ref, held, total, send1, recv1, send2, recv2):
-    me = lax.axis_index("seg")
+def reduce_kernel(n, scale, part_ref, out_ref, held, total, final, send1, recv1, send2, recv2):
+    me = lax.axis_index("seg") // 2
+    core = lax.rem(lax.axis_index("seg"), 2)
 
     def scatter(k):
         to = lax.rem(me + k, n)
@@ -40,18 +41,18 @@
             dst_ref=held.at[k],
             send_sem=send1.at[k],
             recv_sem=recv1.at[k],
-            device_id=(to,),
+            device_id=(2 * to + core,),
             device_id_type=MESH,
         )
 
     def spread(k):
         to = lax.rem(me + k, n)
         return pltpu.make_async_remote_copy(
-            src_ref=total,
+            src_ref=final,
             dst_ref=out_ref.at[me],
             send_sem=send2.at[k],
             recv_sem=recv2.at[k],
-            device_id=(to,),
+            device_id=(2 * to + core,),
             device_id_type=MESH,
         )
 
@@ -66,11 +67,13 @@
         scatter(k).wait_recv()
         total[...] += held[k]
 
+    final[...] = (total[...] * scale).astype(final.dtype)
+
     @pl.loop(1, n)
     def _(k):
         spread(k).start()
 
-    out_ref[me] = total[...]
+    out_ref[me] = final[...]
 
     @pl.loop(1, n)
     def _(k):
@@ -78,17 +81,18 @@
         spread(k).wait()
 
 
-def all_sum(parts):
+def all_sum(parts, scale):
     n = parts.shape[0]
     sems = pltpu.SemaphoreType.DMA((n,))
     return pl.pallas_call(
-        functools.partial(reduce_kernel, n),
-        out_shape=jax.ShapeDtypeStruct(parts.shape, parts.dtype),
+        functools.partial(reduce_kernel, n, scale),
+        out_shape=jax.ShapeDtypeStruct(parts.shape, jnp.bfloat16),
         in_specs=[pl.BlockSpec(memory_space=pltpu.VMEM)],
         out_specs=pl.BlockSpec(memory_space=pltpu.VMEM),
         scratch_shapes=[
             pltpu.VMEM(parts.shape, parts.dtype),
             pltpu.VMEM(parts.shape[1:], parts.dtype),
+            pltpu.VMEM(parts.shape[1:], jnp.bfloat16),
             sems,
             sems,
             sems,
@@ -216,9 +220,21 @@
     part = jnp.dot(own_cols, query_weight, preferred_element_type=jnp.float32)
     blocks = query_width // LANES
     part = jnp.transpose(part.reshape(mem_rows, blocks, LANES), (1, 0, 2))
-    summed = all_sum(part.reshape(n, mem_rows * blocks // n, LANES))
-    summed = jnp.transpose(summed.reshape(blocks, mem_rows, LANES), (1, 0, 2))
-    write_q = (summed.reshape(mem_rows, query_width) * scale).astype(jnp.bfloat16)
+    core = lax.rem(me, 2)
+    pairs = [(i, i + 1 - 2 * (i % 2)) for i in range(n)]
+    share = blocks // 2
+    kept = lax.dynamic_slice_in_dim(part, core * share, share, axis=0)
+    given = lax.dynamic_slice_in_dim(part, (1 - core) * share, share, axis=0)
+    kept = kept + lax.ppermute(given, "seg", pairs)
+    peers = n // 2
+    own_q = all_sum(kept.reshape(peers, mem_rows * share // peers, LANES), scale)
+    own_q = own_q.reshape(share, mem_rows, LANES)
+    other_q = lax.ppermute(own_q, "seg", pairs)
+    low = core == 0
+    write_q = jnp.concatenate(
+        [jnp.where(low, own_q, other_q), jnp.where(low, other_q, own_q)], axis=0
+    )
+    write_q = jnp.transpose(write_q, (1, 0, 2)).reshape(mem_rows, query_width)
 
     own_query, write_q = lax.optimization_barrier((query_weight, write_q))
     query_full = lax.all_gather(own_query, "seg", axis=0, tiled=True)

time: 318 us -> 309 us (0.972)
  Pallas kernels: 77.3 us -> 62.9 us
    pallas_call x1, Pallas kernels: 46.5 us -> 32.1 us  [all_sum(): pl.pallas_call(functools.partial(reduce_kernel, n, scale), out_shape=jax....]
  transfers between devices with their start and end apart: 4 -> 6, of which waited for: 3 -> 5; matrix products, arithmetic and copies ran while one was open for 18% -> 18% of each run, Pallas kernels for 17% -> 13%
where the time goes in v2:
time: 309 us; the launch traced here: 308 us
  waiting for transfers between devices  124 us (40%)
  matrix products  70.3 us (23%)
  Pallas kernels  62.9 us (20%)
  between operations  17 us (6%)
  other arithmetic  16.1 us (5%)
  starting transfers between devices  12.7 us (4%)
  local copies, waits for them, and re-layouts  4.97 us (2%)
    all_gather x1, waiting for transfers between devices, shards(): query_full = lax.all_gather(own_query, 'seg', axis=0, tiled=True)  64.2 us
    all_gather x1, waiting for transfers between devices, shards(): output_full = lax.all_gather(output_weight, 'seg', axis=0, tiled=True)  56.2 us
    pallas_call x1, Pallas kernels, all_sum(): pl.pallas_call(functools.partial(reduce_kernel, n, scale), out_shape=jax....  32.1 us
    dot_general x4, matrix products, finish(): proj = jnp.dot(attn, output_weight, preferred_element_type=jnp.float32)  30.4 us
    pallas_call x4, Pallas kernels, attend(): pl.pallas_call(functools.partial(attend_kernel, first, keys), grid=(KEY_V...  18.4 us
    pallas_call x1, Pallas kernels, small_sum(): pl.pallas_call(functools.partial(total_kernel, n), out_shape=jax.ShapeDty...  12.4 us
    ppermute x2, starting transfers between devices, from_behind(): return lax.ppermute(block, axis, route)  12 us
    dot_general x2, matrix products, shards(): jnp.dot(read_norm, key_matrix, preferred_element_type=jnp.float32)  10.4 us
  transfers between devices with their start and end apart: 6, of which 5 were waited for; matrix products, arithmetic and copies ran while one was open for 18% of the time, Pallas kernels for 13%

profile of v2, /device:TPU:0, one launch (start us, length us, event | category | flops | bytes accessed | tf_op | source)
XLA Modules:
  0.0 308.1 jit_solution(7146340577136018321)
XLA Ops:
  7.2 0.0 all-gather.5.cloned.1.call-start
  7.2 0.7 all-gather.5.cloned.1.call-update
  7.9 0.0 copy-start
  7.9 0.0 copy-start.1
  7.9 0.0 all-gather.3.cloned.1.call-start
  8.0 1.2 convert_element_type.80
  9.2 0.8 dynamic-slice.8
  10.0 1.2 fusion.15
  11.2 0.0 copy-start.8
  11.2 1.3 convolution_bitcast_fusion
  12.5 0.1 copy.19
  12.7 0.1 copy.29
  12.8 0.6 collective-permute-start
  13.3 1.2 collective-permute-done
  14.5 0.8 fusion.21
  15.2 32.1 %query_sum.1 = bf16[16,32,128]{2,1,0:T(8,128)(2,1)} custom-call(f32[16,32,128]{2,1,0:T(8,128)} %bitcast.52), custom_call_target="tpu_custom_call" | custom-call | bytes 30000000 | tf_op jit(solution)/shard_map/query_sum/pallas_call | solution.py:87
  47.3 1.0 copy.15
  48.3 0.1 collective-permute-start.1
  48.4 1.3 collective-permute-done.1
  49.7 1.0 broadcast_select_fusion.3
  50.8 0.8 copy.28
  51.5 0.0 all-gather.3.cloned.1.call-update
  51.6 0.5 fusion
  52.2 0.0 copy-done.8
  52.2 0.0 slice-start.4
  52.2 0.7 fusion.2
  52.9 0.0 copy-start.4
  52.9 0.0 slice-start.5
  52.9 6.8 %convolution_convert_fusion.1.k_ref = bf16[320,1024]{1,0:T(8,128)(2,1)S(1)} fusion(bf16[320,3584]{1,0:T(8,128)(2,1)S(1)} %fusion.2, bf16[3584,1024]{1,0:T(8,128)(2,1)} %param.14), kind=kOutput, calls=%fused_computation.12 | convolution fusion | flops 2349137920 | bytes 10289152 | tf_op jit(solution)/shard_map/dot_general | solution.py:243
  59.8 0.7 slice.17.rk_ref
  60.5 0.0 copy-done.4
  60.5 2.5 convolution_convert_fusion.v_ref
  63.0 0.0 copy-done.2
  63.0 0.7 slice.18.rv_ref
  63.7 0.2 copy-done.3
  63.9 4.5 %attend.4 = bf16[64,2048]{1,0:T(8,128)(2,1)} custom-call(bf16[64,2048]{1,0:T(8,128)(2,1)} %bitcast.46, bf16[64,1024]{1,0:T(8,128)(2,1)} %slice.17.rk_ref, bf16[64,1024]{1,0:T(8,128)(2,1)} %slice.18.rv_ref, bf16[320,1024]{1,0:T(8,128)(2,1)} %copy-done.2, bf16[320,1024]{1,0:T(8,128)(2,1)} %copy-done.3), custom_call_target="tpu_custom_call" | custom-call | flops 201326592 | bytes 6000000 | tf_op jit(solution)/shard_map/attend/pallas_call | solution.py:172
  68.4 56.2 %all-gather.5.cloned.1.call-done = bf16[2048,3584]{1,0:T(8,128)(2,1)} async-done(((bf16[64,3584]{1,0:T(8,128)(2,1)}), bf16[2048,3584]{1,0:T(8,128)(2,1)}) %all-gather.5.cloned.1.call-update) | async-done | bytes 14680080 | tf_op jit(solution)/shard_map/all_gather | solution.py:216
  124.6 8.0 %multiply_reduce_fusion.3 = (f32[64]{0:T(128)S(1)}, f32[64,3584]{1,0:T(8,128)S(1)}) fusion(bf16[64,2048]{1,0:T(8,128)(2,1)} %attend.4, bf16[2048,3584]{1,0:T(8,128)(2,1)} %all-gather.5.cloned.1.call-done), kind=kOutput, calls=%fused_computation.47 | convolution fusion | flops 939982784 | bytes 15859968 | tf_op jit(solution)/shard_map/dot_general | solution.py:192
  132.6 0.2 fusion.16
  132.8 2.4 collective-permute-start.2
  135.8 0.6 collective-permute-done.2
  136.4 0.2 fusion.5
  136.7 5.2 %convolution_convert_fusion.5.rk_ref = bf16[64,1024]{1,0:T(8,128)(2,1)} fusion(bf16[3584,1024]{1,0:T(8,128)(2,1)} %param.14, f32[64]{0:T(128)S(1)} %add_sqrt_fusion.5, f32[3584]{0:T(1024)S(1)} %copy-done.8, bf16[64,3584]{1,0:T(8,128)(2,1)S(1)} %copy-done, bf16[64,3584]{1,0:T(8,128)(2,1)S(1)} %collective-permute-done.2, pred[]{:T(512)S(6)} %eq.7), kind=kOutput, calls=%fused_computation.17 | convolution fusion | flops 470974464 | bytes 8403201 | tf_op jit(solution)/shard_map/dot_general | solution.py:261
  141.9 5.2 %convolution_convert_fusion.4.rv_ref = bf16[64,1024]{1,0:T(8,128)(2,1)} fusion(bf16[3584,1024]{1,0:T(8,128)(2,1)} %param.15, f32[64]{0:T(128)S(1)} %add_sqrt_fusion.5, f32[3584]{0:T(1024)S(1)} %copy-done.8, bf16[64,3584]{1,0:T(8,128)(2,1)S(1)} %copy-done, bf16[64,3584]{1,0:T(8,128)(2,1)S(1)} %collective-permute-done.2, pred[]{:T(512)S(6)} %eq.7), kind=kOutput, calls=%fused_computation.16 | convolution fusion | flops 470974464 | bytes 8403201 | tf_op jit(solution)/shard_map/dot_general | solution.py:264
  147.1 4.5 %attend.5 = bf16[64,2048]{1,0:T(8,128)(2,1)} custom-call(bf16[64,2048]{1,0:T(8,128)(2,1)} %bitcast.47, bf16[64,1024]{1,0:T(8,128)(2,1)} %convolution_convert_fusion.5.rk_ref, bf16[64,1024]{1,0:T(8,128)(2,1)} %convolution_convert_fusion.4.rv_ref, bf16[320,1024]{1,0:T(8,128)(2,1)} %copy-done.2, bf16[320,1024]{1,0:T(8,128)(2,1)} %copy-done.3), custom_call_target="tpu_custom_call" | custom-call | flops 201326592 | bytes 6000000 | tf_op jit(solution)/shard_map/attend/pallas_call | solution.py:172
  151.5 8.2 %multiply_reduce_fusion.2 = (f32[64]{0:T(128)S(1)}, f32[64,3584]{1,0:T(8,128)S(1)}) fusion(bf16[64,2048]{1,0:T(8,128)(2,1)} %attend.5, bf16[2048,3584]{1,0:T(8,128)(2,1)} %all-gather.5.cloned.1.call-done), kind=kOutput, calls=%fused_computation.46 | convolution fusion | flops 939982784 | bytes 15859968 | tf_op jit(solution)/shard_map/dot_general | solution.py:192
  159.8 1.0 fusion.17
  160.8 9.6 %collective-permute-start.3 = (bf16[64,3584]{1,0:T(8,128)(2,1)}, bf16[64,3584]{1,0:T(8,128)(2,1)}, u32[]{:S(2)}, u32[]{:S(2)}) collective-permute-start(bf16[64,3584]{1,0:T(8,128)(2,1)} %fusion.17), channel_id=1, source_target_pairs={{0,1},{1,2},{2,3},{3,4},{4,5},{5,6},{6,7},{7,8},{8,9},{9,10},{10,1... | collective-permute-start | bytes 1376264 | tf_op jit(solution)/shard_map/ppermute | solution.py:24
  170.4 64.2 %all-gather.3.cloned.1.call-done = bf16[3584,2048]{1,0:T(8,128)(2,1)} async-done(((bf16[112,2048]{1,0:T(8,128)(2,1)}), bf16[3584,2048]{1,0:T(8,128)(2,1)}) %all-gather.3.cloned.1.call-update) | async-done | bytes 14680080 | tf_op jit(solution)/shard_map/all_gather | solution.py:240
  234.7 8.5 %fusion.3.q_ref = bf16[256,2048]{1,0:T(8,128)(2,1)} fusion(bf16[3584,2048]{1,0:T(8,128)(2,1)} %all-gather.3.cloned.1.call-done, bf16[320,3584]{1,0:T(8,128)(2,1)S(1)} %copy-done.5), kind=kOutput, calls=%fused_computation.8 | convolution fusion | flops 3759144960 | bytes 17563648 | tf_op jit(solution)/shard_map/dot_general | solution.py:271
  243.2 0.0 collective-permute-done.3
  243.2 0.3 fusion.8
  243.5 5.2 %convolution_convert_fusion.3.rk_ref = bf16[64,1024]{1,0:T(8,128)(2,1)} fusion(bf16[3584,1024]{1,0:T(8,128)(2,1)} %param.14, f32[64]{0:T(128)S(1)} %add_sqrt_fusion.3, f32[3584]{0:T(1024)S(1)} %copy-done.8, bf16[64,3584]{1,0:T(8,128)(2,1)S(1)} %copy-done, bf16[64,3584]{1,0:T(8,128)(2,1)} %collective-permute-done.3, pred[]{:T(512)S(6)} %eq.7), kind=kOutput, calls=%fused_computation.15 | convolution fusion | flops 470974464 | bytes 8403201 | tf_op jit(solution)/shard_map/dot_general | solution.py:261
  248.7 5.2 %convolution_convert_fusion.2.rv_ref = bf16[64,1024]{1,0:T(8,128)(2,1)} fusion(bf16[3584,1024]{1,0:T(8,128)(2,1)} %param.15, f32[64]{0:T(128)S(1)} %add_sqrt_fusion.3, f32[3584]{0:T(1024)S(1)} %copy-done.8, bf16[64,3584]{1,0:T(8,128)(2,1)S(1)} %copy-done, bf16[64,3584]{1,0:T(8,128)(2,1)} %collective-permute-done.3, pred[]{:T(512)S(6)} %eq.7), kind=kOutput, calls=%fused_computation.14 | convolution fusion | flops 470974464 | bytes 8403201 | tf_op jit(solution)/shard_map/dot_general | solution.py:264
  253.8 4.5 %attend.7 = bf16[64,2048]{1,0:T(8,128)(2,1)} custom-call(bf16[64,2048]{1,0:T(8,128)(2,1)} %bitcast.48, bf16[64,1024]{1,0:T(8,128)(2,1)} %convolution_convert_fusion.3.rk_ref, bf16[64,1024]{1,0:T(8,128)(2,1)} %convolution_convert_fusion.2.rv_ref, bf16[320,1024]{1,0:T(8,128)(2,1)} %copy-done.2, bf16[320,1024]{1,0:T(8,128)(2,1)} %copy-done.3), custom_call_target="tpu_custom_call" | custom-call | flops 201326592 | bytes 6000000 | tf_op jit(solution)/shard_map/attend/pallas_call | solution.py:172
  258.3 5.0 %attend.6 = bf16[256,2048]{1,0:T(8,128)(2,1)} custom-call(bf16[256,2048]{1,0:T(8,128)(2,1)} %fusion.3.q_ref, bf16[64,1024]{1,0:T(8,128)(2,1)} %convolution_convert_fusion.3.rk_ref, bf16[64,1024]{1,0:T(8,128)(2,1)} %convolution_convert_fusion.2.rv_ref, bf16[320,1024]{1,0:T(8,128)(2,1)} %copy-done.2, bf16[320,1024]{1,0:T(8,128)(2,1)} %copy-done.3), custom_call_target="tpu_custom_call" | custom-call | flops 671088640 | bytes 6000000 | tf_op jit(solution)/shard_map/attend/pallas_call | solution.py:172
  263.3 11.4 %multiply_reduce_fusion = (f32[256]{0:T(256)S(1)}, f32[256,3584]{1,0:T(8,128)}) fusion(bf16[256,2048]{1,0:T(8,128)(2,1)} %attend.6, bf16[2048,3584]{1,0:T(8,128)(2,1)} %all-gather.5.cloned.1.call-done), kind=kOutput, calls=%fused_computation.6 | convolution fusion | flops 3759931136 | bytes 19399680 | tf_op jit(solution)/shard_map/dot_general | solution.py:192
  274.8 2.7 multiply_reduce_fusion.1
  277.5 3.0 fusion.20
  282.5 0.1 select_maximum_fusion
  282.6 0.6 broadcast_in_dim.2.part_ref
  283.2 12.4 %change_sum.1 = f32[8,128]{1,0:T(8,128)} custom-call(f32[8,128]{1,0:T(8,128)} %broadcast_in_dim.2.part_ref), custom_call_target="tpu_custom_call" | custom-call | bytes 8000000 | tf_op jit(solution)/shard_map/change_sum/pallas_call | solution.py:135
  295.6 1.2 sqrt_bitcast_fusion
  296.8 4.5 %add_convert_fusion = bf16[256,3584]{1,0:T(8,128)(2,1)} fusion(f32[256,3584]{1,0:T(8,128)} %get-tuple-element.20, bf16[256,3584]{1,0:T(8,128)(2,1)} %param.9, f32[3584]{0:T(1024)S(1)} %copy-done.7, f32[256]{0:T(256)S(1)} %add_sqrt_fusion.1), kind=kLoop, calls=%fused_computation.5 | loop fusion | flops 4587520 | bytes 7355392 | tf_op jit(solution)/shard_map/convert_element_type | solution.py:194
  (32 shorter events, 0.2 us)
Async XLA Ops:
  7.2 117.4 %all-gather.5.cloned.1.call-start = ((), (), s32[]{:S(2)}) async-start(), calls=%async_computation.1 | async-start | bytes 15138816 | tf_op jit(solution)/shard_map/all_gather | solution.py:216
  7.9 43.7 %copy-start = (bf16[64,3584]{1,0:T(8,128)(2,1)S(1)}, bf16[64,3584]{1,0:T(8,128)(2,1)}, u32[]{:S(2)}) copy-start(bf16[64,3584]{1,0:T(8,128)(2,1)} %param.10) | copy-start | bytes 1376260
  7.9 43.7 %copy-start.1 = (bf16[256,3584]{1,0:T(8,128)(2,1)S(1)}, bf16[256,3584]{1,0:T(8,128)(2,1)}, u32[]{:S(2)}) copy-start(bf16[256,3584]{1,0:T(8,128)(2,1)} %param.9) | copy-start | bytes 5505028
  7.9 226.7 %all-gather.3.cloned.1.call-start = ((), (), s32[]{:S(2)}) async-start(), calls=%async_computation | async-start | bytes 15138816 | tf_op jit(solution)/shard_map/all_gather | solution.py:240
  11.2 40.9 %copy-start.8 = (f32[3584]{0:T(1024)S(1)}, f32[3584]{0:T(1024)}, u32[]{:S(2)}) copy-start(f32[3584]{0:T(1024)} %param.11) | copy-start | bytes 43012
  12.8 1.7 collective-permute-start
  48.3 1.4 collective-permute-start.1
  52.2 8.3 %slice-start.4 = ((s8[7340032]{0:T(1024)(128)(4,1)}), s8[4194304]{0:T(1024)(128)(4,1)S(1)}, s32[]{:S(2)}) async-start(s8[7340032]{0:T(1024)(128)(4,1)} %bitcast.55), calls=%async_computation.6 | async-start | bytes 8388608
  52.9 7.6 %copy-start.4 = (bf16[320,3584]{1,0:T(8,128)(2,1)}, bf16[320,3584]{1,0:T(8,128)(2,1)S(1)}, u32[]{:S(2)}) copy-start(bf16[320,3584]{1,0:T(8,128)(2,1)S(1)} %fusion.2) | copy-start | bytes 6881284
  52.9 7.6 %slice-start.5 = ((s8[7340032]{0:T(1024)(128)(4,1)}), s8[3145728]{0:T(1024)(128)(4,1)S(1)}, s32[]{:S(2)}) async-start(s8[7340032]{0:T(1024)(128)(4,1)} %bitcast.55), calls=%async_computation.7 | async-start | bytes 6291456
  59.7 3.3 %copy-start.2 = (bf16[320,1024]{1,0:T(8,128)(2,1)}, bf16[320,1024]{1,0:T(8,128)(2,1)S(1)}, u32[]{:S(2)}) copy-start(bf16[320,1024]{1,0:T(8,128)(2,1)S(1)} %convolution_convert_fusion.1.k_ref) | copy-start | bytes 1966084
  63.0 0.9 copy-start.3
  68.4 64.2 %copy-start.7 = (f32[3584]{0:T(1024)S(1)}, f32[3584]{0:T(1024)}, u32[]{:S(2)}) copy-start(f32[3584]{0:T(1024)} %param.12) | copy-start | bytes 43012
  132.8 3.6 %collective-permute-start.2 = (bf16[64,3584]{1,0:T(8,128)(2,1)S(1)}, bf16[64,3584]{1,0:T(8,128)(2,1)S(1)}, u32[]{:S(2)}, u32[]{:S(2)}) collective-permute-start(bf16[64,3584]{1,0:T(8,128)(2,1)S(1)} %fusion.16), channel_id=1, source_target_pairs={{0,1},{1,2},{2,3},{3,4},{4,5},{5,6},{6,7},{7,8},{8,9},{9,10},{10,1... | collective-permute-start | bytes 1376264 | tf_op jit(solution)/shard_map/ppermute | solution.py:24
  151.5 83.1 %copy-start.5 = (bf16[320,3584]{1,0:T(8,128)(2,1)S(1)}, bf16[320,3584]{1,0:T(8,128)(2,1)}, u32[]{:S(2)}) copy-start(bf16[320,3584]{1,0:T(8,128)(2,1)} %copy-done.4) | copy-start | bytes 6881284
  160.8 82.4 %collective-permute-start.3 = (bf16[64,3584]{1,0:T(8,128)(2,1)}, bf16[64,3584]{1,0:T(8,128)(2,1)}, u32[]{:S(2)}, u32[]{:S(2)}) collective-permute-start(bf16[64,3584]{1,0:T(8,128)(2,1)} %fusion.17), channel_id=1, source_target_pairs={{0,1},{1,2},{2,3},{3,4},{4,5},{5,6},{6,7},{7,8},{8,9},{9,10},{10,1... | collective-permute-start | bytes 1376264 | tf_op jit(solution)/shard_map/ppermute | solution.py:24
  258.3 16.4 %slice-start = ((s8[14680064]{0:T(1024)(128)(4,1)}), s8[2097152]{0:T(1024)(128)(4,1)S(1)}, s32[]{:S(2)}) async-start(s8[14680064]{0:T(1024)(128)(4,1)} %bitcast.44), calls=%async_computation.2 | async-start | bytes 4194304
  263.3 11.4 %slice-start.1 = ((s8[14680064]{0:T(1024)(128)(4,1)}), s8[4194304]{0:T(1024)(128)(4,1)S(1)}, s32[]{:S(2)}) async-start(s8[14680064]{0:T(1024)(128)(4,1)} %bitcast.44), calls=%async_computation.3 | async-start | bytes 8388608
  263.3 11.4 %slice-start.2 = ((s8[14680064]{0:T(1024)(128)(4,1)}), s8[4194304]{0:T(1024)(128)(4,1)S(1)}, s32[]{:S(2)}) async-start(s8[14680064]{0:T(1024)(128)(4,1)} %bitcast.44), calls=%async_computation.4 | async-start | bytes 8388608
  263.3 11.4 %slice-start.3 = ((s8[14680064]{0:T(1024)(128)(4,1)}), s8[4194304]{0:T(1024)(128)(4,1)S(1)}, s32[]{:S(2)}) async-start(s8[14680064]{0:T(1024)(128)(4,1)} %bitcast.44), calls=%async_computation.5 | async-start | bytes 8388608
  263.3 11.4 %copy-start.6 = (bf16[64,2048]{1,0:T(8,128)(2,1)S(1)}, bf16[64,2048]{1,0:T(8,128)(2,1)}, u32[]{:S(2)}) copy-start(bf16[64,2048]{1,0:T(8,128)(2,1)} %attend.7) | copy-start | bytes 786436
Sparse Core Ops, SparseCore 0:
  10.8 113.6 all-gather.4
  127.4 107.2 all-gather.2
